TPU v7x, 32 devices: a whole 2x2x4 slice. The times are simulated.
32 devices in a mesh: row: 4 (over x, core), col: 8 (over z, y).
Axes of the slice: x: 2, y: 2, z: 4, core: 2. Of those that a mesh axis runs over, the one named last changes fastest.
Arguments:
- tiles: int32 [4, 8, 8, 128, 128], P('row', 'col'), may hold values from 0 to 1073741823, as said below
- slots: int32 [4, 8, 8], P('row', 'col'), may hold values from 0 to 31, as said below
- factor: float32 [4096, 256], P(('row', 'col')), may hold values from -0.5 to 0.5
- dual: float32 [4096, 256], P(('row', 'col')), may hold values from -0.5 to 0.5
Outputs:
- final_factor: float32 [4096, 256], P(('row', 'col'))
- final_dual: float32 [4096, 256], P(('row', 'col'))
- objective: float32 [3], replicated
- residual: float32 [3], replicated
Inputs may be any that keep to these rules, and one draw needn't show every extreme that they name: `slots`: for every device, 8 distinct block numbers in ascending order. The stored blocks of all devices form a symmetric pattern: the block of rows piece p and columns piece q is stored if and only if the block of rows piece q and columns piece p is; every diagonal block is stored. `tiles`: the stored block of rows piece p and columns piece q is the transpose of the one of rows piece q and columns piece p; diagonal blocks are symmetric.
All inputs are finite; a program needn't handle non-finite values.
Results may differ from a plain program's by a relative error of at most 0.005.
Values may be sent and summed in bfloat16 or wider, within the bound.
A program may use at most 64 MiB of HBM per device.

v0:
```python
import math
import jax
import jax.numpy as jnp
from jax import lax
from jax.sharding import PartitionSpec as P

ITERS = 3
penalty = 2.0
step_size = 0.25
ridge_shift = 0.1
offset = 536870912


def block_weights(integers, vertices):
    unit_scale = math.sqrt(6.0 / vertices) / 2.0**29
    return ((integers - offset).astype(jnp.float32) * unit_scale).astype(jnp.bfloat16)


def unit_rows(values):
    return values * lax.rsqrt(jnp.sum(values * values, axis=1, keepdims=True) + 1e-06)


def local(tiles, slots, factor, dual):
    row_count = lax.axis_size("row")
    col_count = lax.axis_size("col")
    piece_rows = factor.shape[0]
    columns = factor.shape[1]
    vertices = piece_rows * row_count * col_count
    weights = block_weights(tiles.reshape(tiles.shape[2], piece_rows, piece_rows), vertices)
    stored = slots.reshape(-1)
    block_row = stored // row_count
    block_col = stored % row_count

    def combine(partial_value):
        return lax.psum_scatter(partial_value, "col", scatter_dimension=0, tiled=True)

    selector = (block_row[None, :] == jnp.arange(col_count, dtype=jnp.int32)[:, None]).astype(
        jnp.float32
    )
    block_sums = jnp.sum(weights, axis=2, dtype=jnp.float32)
    edge_sums = jnp.dot(selector, block_sums, precision=lax.Precision.HIGHEST)
    degree = combine(edge_sums.reshape(-1))
    current = factor
    lagrange = dual
    projected = unit_rows(current + lagrange / penalty)
    tallies = []
    for iteration in range(ITERS):
        packed = current.astype(jnp.bfloat16)
        own_gram = lax.dot_general(
            packed, packed, (((0,), (0,)), ((), ())), preferred_element_type=jnp.float32
        )
        gram_total = lax.psum(own_gram, ("row", "col"))
        gathered = lax.all_gather(packed, "row", axis=0, tiled=True).reshape(
            -1, piece_rows, columns
        )
        chosen = gathered[block_col]
        products = jnp.einsum("tij,tjk->tik", weights, chosen, preferred_element_type=jnp.float32)
        partial_value = jnp.einsum(
            "at,tik->aik", selector, products, precision=lax.Precision.HIGHEST
        )
        coupled = combine(partial_value.reshape(col_count * piece_rows, columns))
        widened = packed.astype(jnp.float32)
        gradient = degree[:, None] * widened - coupled
        precond = columns / vertices * gram_total + ridge_shift * jnp.eye(
            columns, dtype=jnp.float32
        )
        triangle = jnp.linalg.cholesky(precond)
        descent = 2.0 * gradient - lagrange - penalty * (current - projected)
        current = current + step_size * jax.scipy.linalg.cho_solve((triangle, True), descent.T).T
        projected = unit_rows(current + lagrange / penalty)
        lagrange = lagrange + penalty * (current - projected)
        mismatch = current - projected
        local_sums = jnp.stack([jnp.sum(widened * gradient), jnp.sum(mismatch * mismatch)])
        tallies.append(local_sums)
    stacked = jnp.stack(tallies)
    stacked = lax.psum(stacked, ("row", "col"))
    objective = stacked[:, 0] / (4.0 * vertices)
    residual = stacked[:, 1] / vertices
    return (current, lagrange, objective, residual)


def solution(mesh):
    in_specs = (
        P("row", "col", None, None, None),
        P("row", "col", None),
        P(("row", "col"), None),
        P(("row", "col"), None),
    )
    out_specs = (P(("row", "col"), None), P(("row", "col"), None), P(), P())
    return jax.shard_map(local, mesh=mesh, in_specs=in_specs, out_specs=out_specs, check_vma=False)
```

profile of v0, /device:TPU:0, one launch (start us, length us, event | category | flops | bytes accessed | tf_op | source)
XLA Modules:
  0.0 669.2 jit_solution(12461409791366380685)
XLA Ops:
  10.2 7.2 %all_gather.9 = bf16[512,256]{0,1:T(8,128)(2,1)S(1)} all-gather(bf16[128,256]{0,1:T(8,128)(2,1)S(1)} %get-tuple-element.92), channel_id=1, replica_groups=mesh['row'=4,'col'=8] {'row'}, dimensions={0}, use_global_device_ids=true | all-gather | bytes 327680 | tf_op jit(solution)/shard_map/all_gather | solution.py:53
  21.8 22.3 %all-reduce.1 = f32[1024]{0:T(1024)S(1)} all-reduce(f32[1024]{0:T(1024)S(1)} %convolution_bitcast_fusion), channel_id=2, replica_groups=mesh['row'=4,'col'=8] {'col'}, use_global_device_ids=true, to_apply=%region_6.8.clone | all-reduce | flops 1024 | bytes 8192
  46.1 99.0 %all-reduce.6.cloned.1.call-done = f32[256,256]{0,1:T(8,128)} async-done(((f32[256,256]{0,1:T(8,128)}), f32[256,256]{0,1:T(8,128)}) %all-reduce.6.cloned.1.call-update) | async-done | bytes 262160 | tf_op jit(solution)/shard_map/psum | solution.py:52
  147.1 11.7 %cholesky.172 = f32[128,128]{1,0:T(8,128)S(1)} custom-call(f32[128,128]{1,0:T(8,128)S(1)} %cholesky.270), custom_call_target="Cholesky" | custom-call | tf_op jit(solution)/shard_map/jit(cholesky)/cholesky | solution.py:67
  158.9 9.8 %custom-call.17 = f32[1,128,128]{1,2,0:T(8,128)S(1)} custom-call(f32[1,128,128]{2,1,0:T(8,128)S(1)} %get-tuple-element.104), custom_call_target="InvertDiagBlocksLowerTriangular" | custom-call | tf_op jit(solution)/shard_map/jit(cholesky)/cholesky | solution.py:67
  169.2 11.7 %cholesky.189 = f32[128,128]{1,0:T(8,128)S(1)} custom-call(f32[128,128]{1,0:T(8,128)S(1)} %convolution_subtract_fusion.8), custom_call_target="Cholesky" | custom-call | tf_op jit(solution)/shard_map/jit(cholesky)/cholesky | solution.py:67
  183.0 4.2 while.6
  183.8 1.4 bitcast_dynamic-update-slice_fusion.6
  185.8 1.4 bitcast_dynamic-update-slice_fusion.6
  187.2 19.7 %custom-call.18 = f32[2,128,128]{1,2,0:T(8,128)S(1)} custom-call(f32[2,128,128]{2,1,0:T(8,128)S(1)} %get-tuple-element.26), custom_call_target="InvertDiagBlocksLowerTriangular" | custom-call | tf_op jit(solution)/shard_map/jit(_cho_solve)/triangular_solve | solution.py:69
  209.4 5.8 all_gather.10
  220.1 126.6 %all-reduce.8.cloned.1.call-done = f32[256,256]{0,1:T(8,128)} async-done(((f32[256,256]{0,1:T(8,128)}), f32[256,256]{0,1:T(8,128)}) %all-reduce.8.cloned.1.call-update) | async-done | bytes 262160 | tf_op jit(solution)/shard_map/psum | solution.py:52
  348.7 11.7 %cholesky.206 = f32[128,128]{1,0:T(8,128)S(1)} custom-call(f32[128,128]{1,0:T(8,128)S(1)} %cholesky.273), custom_call_target="Cholesky" | custom-call | tf_op jit(solution)/shard_map/jit(cholesky)/cholesky | solution.py:67
  360.4 9.8 %custom-call.19 = f32[1,128,128]{1,2,0:T(8,128)S(1)} custom-call(f32[1,128,128]{2,1,0:T(8,128)S(1)} %get-tuple-element.100), custom_call_target="InvertDiagBlocksLowerTriangular" | custom-call | tf_op jit(solution)/shard_map/jit(cholesky)/cholesky | solution.py:67
  370.7 11.7 %cholesky.223 = f32[128,128]{1,0:T(8,128)S(1)} custom-call(f32[128,128]{1,0:T(8,128)S(1)} %convolution_subtract_fusion.5), custom_call_target="Cholesky" | custom-call | tf_op jit(solution)/shard_map/jit(cholesky)/cholesky | solution.py:67
  385.1 4.2 while.7
  385.9 1.4 bitcast_dynamic-update-slice_fusion.7
  387.9 1.4 bitcast_dynamic-update-slice_fusion.7
  389.3 19.7 %custom-call.20 = f32[2,128,128]{1,2,0:T(8,128)S(1)} custom-call(f32[2,128,128]{2,1,0:T(8,128)S(1)} %get-tuple-element.27), custom_call_target="InvertDiagBlocksLowerTriangular" | custom-call | tf_op jit(solution)/shard_map/jit(_cho_solve)/triangular_solve | solution.py:69
  409.1 1.6 subtract_bitcast_fusion.1
  413.1 5.8 all_gather.11
  422.7 126.8 %all-reduce.10.cloned.1.call-done = f32[256,256]{0,1:T(8,128)} async-done(((f32[256,256]{0,1:T(8,128)}), f32[256,256]{0,1:T(8,128)}) %all-reduce.10.cloned.1.call-update) | async-done | bytes 262160 | tf_op jit(solution)/shard_map/psum | solution.py:52
  551.5 11.7 %cholesky.240 = f32[128,128]{1,0:T(8,128)S(1)} custom-call(f32[128,128]{1,0:T(8,128)S(1)} %cholesky.276), custom_call_target="Cholesky" | custom-call | tf_op jit(solution)/shard_map/jit(cholesky)/cholesky | solution.py:67
  563.3 9.8 %custom-call.21 = f32[1,128,128]{1,2,0:T(8,128)S(1)} custom-call(f32[1,128,128]{2,1,0:T(8,128)S(1)} %get-tuple-element.96), custom_call_target="InvertDiagBlocksLowerTriangular" | custom-call | tf_op jit(solution)/shard_map/jit(cholesky)/cholesky | solution.py:67
  573.6 11.7 %cholesky.257 = f32[128,128]{1,0:T(8,128)S(1)} custom-call(f32[128,128]{1,0:T(8,128)S(1)} %convolution_subtract_fusion.2), custom_call_target="Cholesky" | custom-call | tf_op jit(solution)/shard_map/jit(cholesky)/cholesky | solution.py:67
  588.0 4.3 while.8
  588.9 1.4 bitcast_dynamic-update-slice_fusion.8
  590.9 1.4 bitcast_dynamic-update-slice_fusion.8
  592.3 19.7 %custom-call.22 = f32[2,128,128]{1,2,0:T(8,128)S(1)} custom-call(f32[2,128,128]{2,1,0:T(8,128)S(1)} %get-tuple-element.28), custom_call_target="InvertDiagBlocksLowerTriangular" | custom-call | tf_op jit(solution)/shard_map/jit(_cho_solve)/triangular_solve | solution.py:69
  612.0 1.7 fusion.7
  619.4 1.4 maximum_bitcast_fusion
  621.5 39.2 %psum.31 = f32[3,2]{1,0:T(4,128)S(1)} all-reduce(f32[3,2]{1,0:T(4,128)S(1)} %pad_maximum_fusion), channel_id=1, replica_groups=mesh['row'=4,'col'=8] {'row','col'}, use_global_device_ids=true, to_apply=%region_22.25 | all-reduce | flops 6 | bytes 48 | tf_op jit(solution)/shard_map/psum | solution.py:76
  (151 shorter events, 42.9 us)
Async XLA Ops:
  8.0 1.1 copy-start.6
  8.0 137.1 %all-reduce.6.cloned.1.call-start = ((), (), s32[]{:S(2)}) async-start(), calls=%async_computation.3 | async-start | bytes 524288 | tf_op jit(solution)/shard_map/psum | solution.py:52
  9.2 8.3 %copy-start.4 = (s32[1,1,8,128,128]{4,3,2,1,0:T(8,128)S(1)}, s32[1,1,8,128,128]{4,3,2,1,0:T(8,128)}, u32[]{:S(2)}) copy-start(s32[1,1,8,128,128]{4,3,2,1,0:T(8,128)} %param.7) | copy-start | bytes 1572868
  10.2 7.3 %copy-start.7 = (s32[1,1,8]{2,1,0:T(1,128)S(1)}, s32[1,1,8]{2,1,0:T(1,128)}, u32[]{:S(2)}) copy-start(s32[1,1,8]{2,1,0:T(1,128)} %param.8) | copy-start | bytes 100
  10.2 196.7 %reduce-scatter.4.cloned.1.call-start = ((), (), s32[]{:S(2)}) async-start(), calls=%async_computation.4 | async-start | bytes 1179648 | tf_op jit(solution)/shard_map/reduce_scatter | solution.py:35
  21.6 325.0 %all-reduce.8.cloned.1.call-start = ((), (), s32[]{:S(2)}) async-start(), calls=%async_computation.5 | async-start | bytes 524288 | tf_op jit(solution)/shard_map/psum | solution.py:52
  44.1 0.7 copy-start.8
  146.1 1.0 copy-start
  219.4 189.6 %reduce-scatter.6.cloned.1.call-start = ((), (), s32[]{:S(2)}) async-start(), calls=%async_computation.6 | async-start | bytes 1179648 | tf_op jit(solution)/shard_map/reduce_scatter | solution.py:35
  220.0 329.5 %all-reduce.10.cloned.1.call-start = ((), (), s32[]{:S(2)}) async-start(), calls=%async_computation.7 | async-start | bytes 524288 | tf_op jit(solution)/shard_map/psum | solution.py:52
  347.6 1.0 copy-start.1
  422.2 189.8 %reduce-scatter.8.cloned.1.call-start = ((), (), s32[]{:S(2)}) async-start(), calls=%async_computation.8 | async-start | bytes 1179648 | tf_op jit(solution)/shard_map/reduce_scatter | solution.py:35
  550.5 1.0 copy-start.2
  587.9 24.1 %copy-start.5 = (f32[128,256]{0,1:T(8,128)S(1)}, f32[128,256]{0,1:T(8,128)}, u32[]{:S(2)}) copy-start(f32[128,256]{0,1:T(8,128)} %reduce-scatter.4.cloned.1.call-done) | copy-start | bytes 393220
  588.0 24.0 %copy-start.3 = (f32[128,256]{0,1:T(8,128)S(1)}, f32[128,256]{0,1:T(8,128)}, u32[]{:S(2)}) copy-start(f32[128,256]{0,1:T(8,128)} %reduce-scatter.6.cloned.1.call-done) | copy-start | bytes 393220
Sparse Core Ops, SparseCore 0:
  14.3 130.7 all-reduce.5
  219.5 127.0 all-reduce.7
  422.3 127.1 all-reduce.9
Sparse Core Ops, SparseCore 1:
  21.7 66.1 reduce-scatter.3
  223.3 63.7 reduce-scatter.5
  426.0 63.8 reduce-scatter.7
where the time goes:
time: 673 us; the launch traced here: 669 us
  waiting for transfers between devices  354 us (53%)
  other arithmetic  176 us (26%)
  blocking collectives  80.4 us (12%)
  local copies, waits for them, and re-layouts  25.8 us (4%)
  between operations  21.1 us (3%)
  matrix products  11.9 us (2%)
    psum x3, waiting for transfers between devices, local(): gram_total = lax.psum(own_gram, ('row', 'col'))  352 us
    another operation x20, other arithmetic, local(): triangle = jnp.linalg.cholesky(precond)  103 us
    another operation x7, other arithmetic, local(): jax.scipy.linalg.cho_solve((triangle, True), descent.T)  59.1 us
    psum x1, blocking collectives, local(): stacked = lax.psum(stacked, ('row', 'col'))  39.2 us
    unnamed x1, blocking collectives  22.3 us
    all_gather x3, blocking collectives, local(): lax.all_gather(packed, 'row', axis=0, tiled=True)  18.8 us
  transfers between devices with their start and end apart: 6, of which 3 were waited for; matrix products, arithmetic and copies ran while one was open for 27% of the time, Pallas kernels for 0%

commit v1 on v0

--- a/solution.py
+++ b/solution.py
@@ -49,7 +49,9 @@
         own_gram = lax.dot_general(
             packed, packed, (((0,), (0,)), ((), ())), preferred_element_type=jnp.float32
         )
-        gram_total = lax.psum(own_gram, ("row", "col"))
+        gram_total = own_gram
+        for over in ("col", "row"):
+            gram_total = lax.psum(gram_total, over)
         gathered = lax.all_gather(packed, "row", axis=0, tiled=True).reshape(
             -1, piece_rows, columns
         )

time: 673 us -> 615 us (0.914)
  waiting for transfers between devices: 354 us -> 299 us
    psum x3 -> x6, waiting for transfers between devices: 352 us -> 278 us  [local(): gram_total = lax.psum(gram_total, over)]
    reduce_scatter x3, waiting for transfers between devices: 0.08 us -> 19.2 us  [combine(): lax.psum_scatter(partial_value, 'col', scatter_dimension=0, tiled=True)]
  transfers between devices with their start and end apart: 6 -> 9, of which waited for: 3 -> 9; matrix products, arithmetic and copies ran while one was open for 27% -> 31% of each run, Pallas kernels for 0% -> 0%
where the time goes in v1:
time: 615 us; the launch traced here: 612 us
  waiting for transfers between devices  299 us (49%)
  other arithmetic  176 us (29%)
  blocking collectives  78.9 us (13%)
  local copies, waits for them, and re-layouts  25.8 us (4%)
  between operations  19.5 us (3%)
  matrix products  11.8 us (2%)
    psum x6, waiting for transfers between devices, local(): gram_total = lax.psum(gram_total, over)  278 us
    another operation x20, other arithmetic, local(): triangle = jnp.linalg.cholesky(precond)  103 us
    another operation x7, other arithmetic, local(): jax.scipy.linalg.cho_solve((triangle, True), descent.T)  59.1 us
    psum x1, blocking collectives, local(): stacked = lax.psum(stacked, ('row', 'col'))  39.9 us
    unnamed x1, blocking collectives  20.1 us
    reduce_scatter x3, waiting for transfers between devices, combine(): lax.psum_scatter(partial_value, 'col', scatter_dimension=0, tiled=True)  19.2 us
    all_gather x3, blocking collectives, local(): lax.all_gather(packed, 'row', axis=0, tiled=True)  18.8 us
  transfers between devices with their start and end apart: 9, of which 9 were waited for; matrix products, arithmetic and copies ran while one was open for 31% of the time, Pallas kernels for 0%

profile of v1, /device:TPU:0, one launch (start us, length us, event | category | flops | bytes accessed | tf_op | source)
XLA Modules:
  0.0 611.6 jit_solution(6509748193314757352)
XLA Ops:
  9.4 7.2 %all_gather.9 = bf16[512,256]{0,1:T(8,128)(2,1)S(1)} all-gather(bf16[128,256]{0,1:T(8,128)(2,1)S(1)} %get-tuple-element.92), channel_id=1, replica_groups=mesh['row'=4,'col'=8] {'row'}, dimensions={0}, use_global_device_ids=true | all-gather | bytes 327680 | tf_op jit(solution)/shard_map/all_gather | solution.py:55
  17.9 67.2 %all-reduce.9.cloned.1.call-done = f32[256,256]{0,1:T(8,128)} async-done(((f32[256,256]{0,1:T(8,128)}), f32[256,256]{0,1:T(8,128)}) %all-reduce.9.cloned.1.call-update) | async-done | bytes 262160 | tf_op jit(solution)/shard_map/psum | solution.py:54
  88.2 20.1 %all-reduce.1 = f32[1024]{0:T(1024)S(1)} all-reduce(f32[1024]{0:T(1024)S(1)} %convolution_bitcast_fusion), channel_id=2, replica_groups=mesh['row'=4,'col'=8] {'col'}, use_global_device_ids=true, to_apply=%region_7.9.clone | all-reduce | flops 1024 | bytes 8192
  110.3 8.6 %all-reduce.11.cloned.1.call-done = f32[256,256]{0,1:T(8,128)} async-done(((f32[256,256]{0,1:T(8,128)}), f32[256,256]{0,1:T(8,128)}) %all-reduce.11.cloned.1.call-update) | async-done | bytes 262160 | tf_op jit(solution)/shard_map/psum | solution.py:54
  120.9 11.7 %cholesky.172 = f32[128,128]{1,0:T(8,128)S(1)} custom-call(f32[128,128]{1,0:T(8,128)S(1)} %cholesky.270), custom_call_target="Cholesky" | custom-call | tf_op jit(solution)/shard_map/jit(cholesky)/cholesky | solution.py:69
  132.7 9.8 %custom-call.17 = f32[1,128,128]{1,2,0:T(8,128)S(1)} custom-call(f32[1,128,128]{2,1,0:T(8,128)S(1)} %get-tuple-element.104), custom_call_target="InvertDiagBlocksLowerTriangular" | custom-call | tf_op jit(solution)/shard_map/jit(cholesky)/cholesky | solution.py:69
  143.0 11.7 %cholesky.189 = f32[128,128]{1,0:T(8,128)S(1)} custom-call(f32[128,128]{1,0:T(8,128)S(1)} %convolution_subtract_fusion.8), custom_call_target="Cholesky" | custom-call | tf_op jit(solution)/shard_map/jit(cholesky)/cholesky | solution.py:69
  156.8 4.2 while.6
  161.0 19.7 %custom-call.18 = f32[2,128,128]{1,2,0:T(8,128)S(1)} custom-call(f32[2,128,128]{2,1,0:T(8,128)S(1)} %get-tuple-element.26), custom_call_target="InvertDiagBlocksLowerTriangular" | custom-call | tf_op jit(solution)/shard_map/jit(_cho_solve)/triangular_solve | solution.py:71
  180.7 6.9 %reduce-scatter.4.cloned.1.call-done = f32[128,256]{0,1:T(8,128)} async-done(((f32[1024,256]{0,1:T(8,128)}), f32[128,256]{0,1:T(8,128)}) %reduce-scatter.4.cloned.1.call-update) | async-done | bytes 131088 | tf_op jit(solution)/shard_map/reduce_scatter | solution.py:35
  190.1 5.8 all_gather.10
  200.1 68.2 %all-reduce.13.cloned.1.call-done = f32[256,256]{0,1:T(8,128)} async-done(((f32[256,256]{0,1:T(8,128)}), f32[256,256]{0,1:T(8,128)}) %all-reduce.13.cloned.1.call-update) | async-done | bytes 262160 | tf_op jit(solution)/shard_map/psum | solution.py:54
  269.0 33.0 %all-reduce.15.cloned.1.call-done = f32[256,256]{0,1:T(8,128)} async-done(((f32[256,256]{0,1:T(8,128)}), f32[256,256]{0,1:T(8,128)}) %all-reduce.15.cloned.1.call-update) | async-done | bytes 262160 | tf_op jit(solution)/shard_map/psum | solution.py:54
  304.0 11.7 %cholesky.206 = f32[128,128]{1,0:T(8,128)S(1)} custom-call(f32[128,128]{1,0:T(8,128)S(1)} %cholesky.273), custom_call_target="Cholesky" | custom-call | tf_op jit(solution)/shard_map/jit(cholesky)/cholesky | solution.py:69
  315.8 9.8 %custom-call.19 = f32[1,128,128]{1,2,0:T(8,128)S(1)} custom-call(f32[1,128,128]{2,1,0:T(8,128)S(1)} %get-tuple-element.100), custom_call_target="InvertDiagBlocksLowerTriangular" | custom-call | tf_op jit(solution)/shard_map/jit(cholesky)/cholesky | solution.py:69
  326.1 11.7 %cholesky.223 = f32[128,128]{1,0:T(8,128)S(1)} custom-call(f32[128,128]{1,0:T(8,128)S(1)} %convolution_subtract_fusion.5), custom_call_target="Cholesky" | custom-call | tf_op jit(solution)/shard_map/jit(cholesky)/cholesky | solution.py:69
  340.5 4.2 while.7
  344.7 19.7 %custom-call.20 = f32[2,128,128]{1,2,0:T(8,128)S(1)} custom-call(f32[2,128,128]{2,1,0:T(8,128)S(1)} %get-tuple-element.27), custom_call_target="InvertDiagBlocksLowerTriangular" | custom-call | tf_op jit(solution)/shard_map/jit(_cho_solve)/triangular_solve | solution.py:71
  364.4 6.2 %reduce-scatter.6.cloned.1.call-done = f32[128,256]{0,1:T(8,128)} async-done(((f32[1024,256]{0,1:T(8,128)}), f32[128,256]{0,1:T(8,128)}) %reduce-scatter.6.cloned.1.call-update) | async-done | bytes 131088 | tf_op jit(solution)/shard_map/reduce_scatter | solution.py:35
  370.6 1.6 subtract_bitcast_fusion.1
  374.6 5.8 all_gather.11
  383.7 68.3 %all-reduce.17.cloned.1.call-done = f32[256,256]{0,1:T(8,128)} async-done(((f32[256,256]{0,1:T(8,128)}), f32[256,256]{0,1:T(8,128)}) %all-reduce.17.cloned.1.call-update) | async-done | bytes 262160 | tf_op jit(solution)/shard_map/psum | solution.py:54
  452.8 33.1 %all-reduce.19.cloned.1.call-done = f32[256,256]{0,1:T(8,128)} async-done(((f32[256,256]{0,1:T(8,128)}), f32[256,256]{0,1:T(8,128)}) %all-reduce.19.cloned.1.call-update) | async-done | bytes 262160 | tf_op jit(solution)/shard_map/psum | solution.py:54
  487.9 11.7 %cholesky.240 = f32[128,128]{1,0:T(8,128)S(1)} custom-call(f32[128,128]{1,0:T(8,128)S(1)} %cholesky.276), custom_call_target="Cholesky" | custom-call | tf_op jit(solution)/shard_map/jit(cholesky)/cholesky | solution.py:69
  499.7 9.8 %custom-call.21 = f32[1,128,128]{1,2,0:T(8,128)S(1)} custom-call(f32[1,128,128]{2,1,0:T(8,128)S(1)} %get-tuple-element.96), custom_call_target="InvertDiagBlocksLowerTriangular" | custom-call | tf_op jit(solution)/shard_map/jit(cholesky)/cholesky | solution.py:69
  510.0 11.7 %cholesky.257 = f32[128,128]{1,0:T(8,128)S(1)} custom-call(f32[128,128]{1,0:T(8,128)S(1)} %convolution_subtract_fusion.2), custom_call_target="Cholesky" | custom-call | tf_op jit(solution)/shard_map/jit(cholesky)/cholesky | solution.py:69
  524.4 4.3 while.8
  527.2 1.4 bitcast_dynamic-update-slice_fusion.8
  528.6 19.7 %custom-call.22 = f32[2,128,128]{1,2,0:T(8,128)S(1)} custom-call(f32[2,128,128]{2,1,0:T(8,128)S(1)} %get-tuple-element.28), custom_call_target="InvertDiagBlocksLowerTriangular" | custom-call | tf_op jit(solution)/shard_map/jit(_cho_solve)/triangular_solve | solution.py:71
  548.3 6.2 %reduce-scatter.8.cloned.1.call-done = f32[128,256]{0,1:T(8,128)} async-done(((f32[1024,256]{0,1:T(8,128)}), f32[128,256]{0,1:T(8,128)}) %reduce-scatter.8.cloned.1.call-update) | async-done | bytes 131088 | tf_op jit(solution)/shard_map/reduce_scatter | solution.py:35
  554.5 1.7 fusion.7
  564.0 39.9 %psum.55 = f32[3,2]{1,0:T(4,128)S(1)} all-reduce(f32[3,2]{1,0:T(4,128)S(1)} %pad_maximum_fusion), channel_id=1, replica_groups=mesh['row'=4,'col'=8] {'row','col'}, use_global_device_ids=true, to_apply=%region_25.28 | all-reduce | flops 6 | bytes 48 | tf_op jit(solution)/shard_map/psum | solution.py:78
  (160 shorter events, 51.4 us)
Async XLA Ops:
  7.2 1.1 copy-start.6
  7.2 77.9 %all-reduce.9.cloned.1.call-start = ((), (), s32[]{:S(2)}) async-start(), calls=%async_computation.3 | async-start | bytes 524288 | tf_op jit(solution)/shard_map/psum | solution.py:54
  8.4 8.2 %copy-start.4 = (s32[1,1,8,128,128]{4,3,2,1,0:T(8,128)S(1)}, s32[1,1,8,128,128]{4,3,2,1,0:T(8,128)}, u32[]{:S(2)}) copy-start(s32[1,1,8,128,128]{4,3,2,1,0:T(8,128)} %param.7) | copy-start | bytes 1572868
  9.3 7.3 %copy-start.7 = (s32[1,1,8]{2,1,0:T(1,128)S(1)}, s32[1,1,8]{2,1,0:T(1,128)}, u32[]{:S(2)}) copy-start(s32[1,1,8]{2,1,0:T(1,128)} %param.8) | copy-start | bytes 100
  9.3 109.6 %all-reduce.11.cloned.1.call-start = ((), (), s32[]{:S(2)}) async-start(), calls=%async_computation.4 | async-start | bytes 524288 | tf_op jit(solution)/shard_map/psum | solution.py:54
  85.1 102.5 %reduce-scatter.4.cloned.1.call-start = ((), (), s32[]{:S(2)}) async-start(), calls=%async_computation.5 | async-start | bytes 1179648 | tf_op jit(solution)/shard_map/reduce_scatter | solution.py:35
  88.0 180.3 %all-reduce.13.cloned.1.call-start = ((), (), s32[]{:S(2)}) async-start(), calls=%async_computation.6 | async-start | bytes 524288 | tf_op jit(solution)/shard_map/psum | solution.py:54
  108.4 0.7 copy-start.8
  119.9 1.0 copy-start
  198.2 103.8 %all-reduce.15.cloned.1.call-start = ((), (), s32[]{:S(2)}) async-start(), calls=%async_computation.7 | async-start | bytes 524288 | tf_op jit(solution)/shard_map/psum | solution.py:54
  268.4 102.2 %reduce-scatter.6.cloned.1.call-start = ((), (), s32[]{:S(2)}) async-start(), calls=%async_computation.8 | async-start | bytes 1179648 | tf_op jit(solution)/shard_map/reduce_scatter | solution.py:35
  269.0 183.1 %all-reduce.17.cloned.1.call-start = ((), (), s32[]{:S(2)}) async-start(), calls=%async_computation.9 | async-start | bytes 524288 | tf_op jit(solution)/shard_map/psum | solution.py:54
  303.0 1.0 copy-start.1
  381.9 104.0 %all-reduce.19.cloned.1.call-start = ((), (), s32[]{:S(2)}) async-start(), calls=%async_computation.10 | async-start | bytes 524288 | tf_op jit(solution)/shard_map/psum | solution.py:54
  452.1 102.4 %reduce-scatter.8.cloned.1.call-start = ((), (), s32[]{:S(2)}) async-start(), calls=%async_computation.11 | async-start | bytes 1179648 | tf_op jit(solution)/shard_map/reduce_scatter | solution.py:35
  486.9 1.0 copy-start.2
  524.3 30.2 %copy-start.5 = (f32[128,256]{0,1:T(8,128)S(1)}, f32[128,256]{0,1:T(8,128)}, u32[]{:S(2)}) copy-start(f32[128,256]{0,1:T(8,128)} %reduce-scatter.4.cloned.1.call-done) | copy-start | bytes 393220
  524.3 30.1 %copy-start.3 = (f32[128,256]{0,1:T(8,128)S(1)}, f32[128,256]{0,1:T(8,128)}, u32[]{:S(2)}) copy-start(f32[128,256]{0,1:T(8,128)} %reduce-scatter.6.cloned.1.call-done) | copy-start | bytes 393220
Sparse Core Ops, SparseCore 0:
  11.3 73.7 all-reduce.8
  87.4 31.4 all-reduce.10
  122.3 65.1 reduce-scatter.3
  198.4 69.9 all-reduce.12
  270.5 31.4 all-reduce.14
  305.3 65.2 reduce-scatter.5
  382.0 70.0 all-reduce.16
  454.4 31.4 all-reduce.18
  489.3 65.1 reduce-scatter.7
